TPU v7x, 32 devices: a whole 2x2x4 slice. The times are simulated.
32 devices in a mesh: tok: 16 (over z, y, core), lay: 2 (over x).
Axes of the slice: x: 2, y: 2, z: 4, core: 2. Of those that a mesh axis runs over, the one named last changes fastest.
Arguments:
- first_acts: bfloat16 [2, 4096, 5120], P('lay', 'tok'), may hold values from -40 to 40
- second_acts: bfloat16 [2, 4096, 5120], P('lay', 'tok'), may hold values from -40 to 40
Outputs:
- whitening: float32 [2, 2, 40, 128, 128], P(None, 'lay')
- similarity: float32 [2, 2, 40], P('lay')
All inputs are finite; a program needn't handle non-finite values.
Results may differ from a plain program's by a relative error of at most 0.0003.
Values may be sent and summed in bfloat16 or wider, within the bound.
A program may use at most 128 MiB of HBM per device.

v0:
```python
import jax
import jax.numpy as jnp
from jax import lax
from jax.sharding import PartitionSpec as P

HEADS = 40
HEAD_DIM = 128
ITERS = 6


ridge_weight = 0.05
top_precision = lax.Precision.HIGHEST


def newton_whiten(matrices):
    unit_matrix = jnp.eye(HEAD_DIM, dtype=jnp.float32)
    scale_norm = jnp.sqrt(jnp.sum(matrices * matrices, axis=(-2, -1), keepdims=True))
    square_iter = matrices / scale_norm
    inverse_iter = jnp.broadcast_to(unit_matrix, matrices.shape)
    for sweep_index in range(ITERS):
        factor_iter = 1.5 * unit_matrix - 0.5 * jnp.matmul(
            inverse_iter, square_iter, precision=top_precision
        )
        square_iter = jnp.matmul(square_iter, factor_iter, precision=top_precision)
        inverse_iter = jnp.matmul(factor_iter, inverse_iter, precision=top_precision)
    return inverse_iter / jnp.sqrt(scale_norm)


def covariance(gram_total, col_sums, token_total):
    unit_matrix = jnp.eye(HEAD_DIM, dtype=jnp.float32)
    column_mean = col_sums / token_total
    return (
        gram_total / token_total
        - column_mean[..., :, None] * column_mean[..., None, :]
        + ridge_weight * unit_matrix
    )


def partial_stats(act_block, token_rows):
    shaped = act_block.reshape(act_block.shape[0], token_rows, HEADS, HEAD_DIM)
    gram_part = jnp.einsum("lthi,lthj->lhij", shaped, shaped, preferred_element_type=jnp.float32)
    col_sums = jnp.sum(shaped, axis=1, dtype=jnp.float32)
    return (gram_part, col_sums)


def local(first_acts, second_acts):
    lay_dev = first_acts.shape[0]
    token_rows = first_acts.shape[1]
    token_total = token_rows * lax.axis_size("tok")
    gathered = lax.all_gather(second_acts, "lay", axis=0, tiled=True)
    gram_first, sums_first = partial_stats(first_acts, token_rows)
    gram_second, sums_second = partial_stats(second_acts, token_rows)
    gram_total, sums_total = lax.psum(
        (jnp.stack([gram_first, gram_second]), jnp.stack([sums_first, sums_second])), "tok"
    )
    whitening = newton_whiten(covariance(gram_total, sums_total, token_total))
    white_first = whitening[0]
    sums_first = sums_total[0]
    white_second, sums_second = (
        lax.all_gather(whitening[1], "lay", axis=0, tiled=True),
        lax.all_gather(sums_total[1], "lay", axis=0, tiled=True),
    )
    mean_first = sums_first / token_total
    mean_second = sums_second / token_total
    view_first = first_acts.reshape(lay_dev, token_rows, HEADS, HEAD_DIM)
    view_second = gathered.reshape(gathered.shape[0], token_rows, HEADS, HEAD_DIM)
    cross_part = jnp.einsum(
        "athi,bthj->abhij", view_first, view_second, preferred_element_type=jnp.float32
    )
    left_product = jnp.matmul(
        white_first[:, None], cross_part / token_total, precision=top_precision
    )
    whitened_part = jnp.matmul(left_product, white_second[None], precision=top_precision)
    row_share = HEAD_DIM // lax.axis_size("tok")
    row_block = lax.psum_scatter(whitened_part, "tok", scatter_dimension=3, tiled=True)
    proj_first = jnp.einsum("ahij,ahj->ahi", white_first, mean_first, precision=top_precision)
    proj_second = jnp.einsum("bhi,bhij->bhj", mean_second, white_second, precision=top_precision)
    proj_rows = lax.dynamic_slice_in_dim(
        proj_first, lax.axis_index("tok") * row_share, row_share, 2
    )
    row_block = row_block - proj_rows[:, None, :, :, None] * proj_second[None, :, :, None, :]
    similarity = lax.psum(jnp.sum(row_block * row_block, axis=(-2, -1)), "tok") / HEAD_DIM
    return (whitening, similarity)


def solution(mesh):
    in_specs = (P("lay", "tok", None), P("lay", "tok", None))
    out_specs = (P(None, "lay", None, None, None), P("lay", None, None))
    return jax.shard_map(local, mesh=mesh, in_specs=in_specs, out_specs=out_specs, check_vma=False)
```

profile of v0, /device:TPU:0, one launch (start us, length us, event | category | flops | bytes accessed | tf_op | source)
XLA Modules:
  0.0 469.5 jit_solution(36682492622054432)
XLA Ops:
  8.1 2.4 copy.36
  13.2 3.0 pad_maximum_fusion
  19.7 64.8 %psum.22 = f32[2,1,40,128]{3,2,1,0:T(8,128)S(1)} all-reduce(f32[2,1,40,128]{3,2,1,0:T(8,128)S(1)} %pad_maximum_fusion.1), channel_id=1, replica_groups=mesh['tok'=16,'lay'=2] {'tok'}, use_global_device_ids=true, to_apply=%region_3.0 | all-reduce | flops 10240 | bytes 81920 | tf_op jit(solution)/shard_map/psum | solution.py:53
  84.5 60.2 %all-reduce.2.cloned.1.call-done = f32[2,1,40,128,128]{4,3,2,1,0:T(8,128)} async-done(((f32[2,1,40,128,128]{4,3,2,1,0:T(8,128)}), f32[2,1,40,128,128]{4,3,2,1,0:T(8,128)}) %all-reduce.2.cloned.1.call-update) | async-done | bytes 5242896 | tf_op jit(solution)/shard_map/psum | solution.py:53
  144.7 5.5 %multiply_reduce_fusion = f32[2,40]{1,0:T(2,128)S(1)} fusion(f32[2,1,40,128,128]{4,3,2,1,0:T(8,128)} %all-reduce.2.cloned.1.call-done, f32[128,128]{1,0:T(8,128)S(1)} %fusion.74, f32[2,40,128]{2,1,0:T(8,128)S(1)} %multiply_bitcast_fusion.1), kind=kLoop, calls=%fused_computation.20 | loop fusion | flops 7864240 | bytes 5349696 | tf_op jit(solution)/shard_map/reduce_sum | solution.py:17
  150.2 5.8 %fusion.6 = f32[2,40,128,128]{3,2,1,0:T(8,128)S(1)} fusion(f32[128,128]{1,0:T(8,128)S(1)} %fusion.75, f32[2,1,40,128,128]{4,3,2,1,0:T(8,128)S(1)} %copy-done.4, f32[2,40]{1,0:T(2,128)S(1)} %get-tuple-element.10, f32[128,128]{1,0:T(8,128)S(1)} %fusion.74, f32[2,40,128]{2,1,0:T(8,128)S(1)} %multiply_bitcast_fusion.1), kind=kOutput, calls=%fused_computation.7 | convolution fusion | flops 2019819520 | bytes 10658112 | tf_op jit(solution)/shard_map/dot_general | solution.py:21
  156.1 5.4 %fusion.13 = f32[2,40,128,128]{3,2,1,0:T(8,128)S(1)} fusion(f32[2,40,128,128]{3,2,1,0:T(8,128)S(1)} %fusion.6, f32[128,128]{1,0:T(8,128)S(1)} %fusion.75, f32[128,128]{1,0:T(8,128)S(1)} %fusion.76), kind=kOutput, calls=%fused_computation.24 | convolution fusion | flops 2015887360 | bytes 10616832 | tf_op jit(solution)/shard_map/dot_general | solution.py:25
  161.5 7.9 %fusion.4 = f32[2,40,128,128]{3,2,1,0:T(8,128)S(1)} fusion(f32[2,40,128,128]{3,2,1,0:T(8,128)S(1)} %fusion.6, f32[128,128]{1,0:T(8,128)S(1)} %fusion.76, f32[2,1,40,128,128]{4,3,2,1,0:T(8,128)S(1)} %copy-done.4, f32[2,40]{1,0:T(2,128)S(1)} %get-tuple-element.10, f32[128,128]{1,0:T(8,128)S(1)} %fusion.74, f32[2,40,128]{2,1,0:T(8,128)S(1)} %multiply_bitcast_fusion.1), kind=kOutput, calls=%fused_computation.5 | convolution fusion | flops 2022440960 | bytes 15900992 | tf_op jit(solution)/shard_map/dot_general | solution.py:24
  169.4 7.0 %fusion.91 = f32[2,40,128,128]{3,2,1,0:T(8,128)S(1)} fusion(f32[2,40,128,128]{3,2,1,0:T(8,128)S(1)} %fusion.13, f32[2,40,128,128]{3,2,1,0:T(8,128)S(1)} %fusion.4), kind=kOutput, calls=%fused_computation.98 | convolution fusion | flops 2013265920 | bytes 15728640 | tf_op jit(solution)/shard_map/dot_general | solution.py:21
  176.4 7.2 %fusion.14 = f32[2,40,128,128]{3,2,1,0:T(8,128)S(1)} fusion(f32[2,40,128,128]{3,2,1,0:T(8,128)S(1)} %fusion.4, f32[2,40,128,128]{3,2,1,0:T(8,128)S(1)} %fusion.91, f32[128,128]{1,0:T(8,128)S(1)} %fusion.76), kind=kOutput, calls=%fused_computation.25 | convolution fusion | flops 2015887360 | bytes 15794176 | tf_op jit(solution)/shard_map/dot_general | solution.py:24
  183.6 7.4 %fusion.15 = f32[2,40,128,128]{3,2,1,0:T(8,128)S(1)} fusion(f32[2,40,128,128]{3,2,1,0:T(8,128)S(1)} %fusion.13, f32[2,40,128,128]{3,2,1,0:T(8,128)S(1)} %fusion.91, f32[128,128]{1,0:T(8,128)S(1)} %fusion.76), kind=kOutput, calls=%fused_computation.26 | convolution fusion | flops 2015887360 | bytes 15794176 | tf_op jit(solution)/shard_map/dot_general | solution.py:25
  191.1 7.0 %fusion.92 = f32[2,40,128,128]{3,2,1,0:T(8,128)S(1)} fusion(f32[2,40,128,128]{3,2,1,0:T(8,128)S(1)} %fusion.15, f32[2,40,128,128]{3,2,1,0:T(8,128)S(1)} %fusion.14), kind=kOutput, calls=%fused_computation.99 | convolution fusion | flops 2013265920 | bytes 15728640 | tf_op jit(solution)/shard_map/dot_general | solution.py:21
  198.1 7.0 %fusion.16 = f32[2,40,128,128]{3,2,1,0:T(8,128)S(1)} fusion(f32[2,40,128,128]{3,2,1,0:T(8,128)S(1)} %fusion.14, f32[2,40,128,128]{3,2,1,0:T(8,128)S(1)} %fusion.92, f32[128,128]{1,0:T(8,128)S(1)} %fusion.76), kind=kOutput, calls=%fused_computation.27 | convolution fusion | flops 2015887360 | bytes 15794176 | tf_op jit(solution)/shard_map/dot_general | solution.py:24
  205.1 7.1 %fusion.17 = f32[2,40,128,128]{3,2,1,0:T(8,128)S(1)} fusion(f32[2,40,128,128]{3,2,1,0:T(8,128)S(1)} %fusion.15, f32[2,40,128,128]{3,2,1,0:T(8,128)S(1)} %fusion.92, f32[128,128]{1,0:T(8,128)S(1)} %fusion.76), kind=kOutput, calls=%fused_computation.28 | convolution fusion | flops 2015887360 | bytes 15794176 | tf_op jit(solution)/shard_map/dot_general | solution.py:25
  212.3 6.9 %fusion.93 = f32[2,40,128,128]{3,2,1,0:T(8,128)S(1)} fusion(f32[2,40,128,128]{3,2,1,0:T(8,128)S(1)} %fusion.17, f32[2,40,128,128]{3,2,1,0:T(8,128)S(1)} %fusion.16), kind=kOutput, calls=%fused_computation.100 | convolution fusion | flops 2013265920 | bytes 15728640 | tf_op jit(solution)/shard_map/dot_general | solution.py:21
  219.1 6.9 %fusion.18 = f32[2,40,128,128]{3,2,1,0:T(8,128)S(1)} fusion(f32[2,40,128,128]{3,2,1,0:T(8,128)S(1)} %fusion.16, f32[2,40,128,128]{3,2,1,0:T(8,128)S(1)} %fusion.93, f32[128,128]{1,0:T(8,128)S(1)} %fusion.76), kind=kOutput, calls=%fused_computation.29 | convolution fusion | flops 2015887360 | bytes 15794176 | tf_op jit(solution)/shard_map/dot_general | solution.py:24
  226.0 7.5 %fusion.19 = f32[2,40,128,128]{3,2,1,0:T(8,128)S(1)} fusion(f32[2,40,128,128]{3,2,1,0:T(8,128)S(1)} %fusion.17, f32[2,40,128,128]{3,2,1,0:T(8,128)S(1)} %fusion.93, f32[128,128]{1,0:T(8,128)S(1)} %fusion.76), kind=kOutput, calls=%fused_computation.30 | convolution fusion | flops 2015887360 | bytes 15794176 | tf_op jit(solution)/shard_map/dot_general | solution.py:25
  233.5 6.7 %fusion.94 = f32[2,40,128,128]{3,2,1,0:T(8,128)S(1)} fusion(f32[2,40,128,128]{3,2,1,0:T(8,128)S(1)} %fusion.19, f32[2,40,128,128]{3,2,1,0:T(8,128)S(1)} %fusion.18), kind=kOutput, calls=%fused_computation.101 | convolution fusion | flops 2013265920 | bytes 15728640 | tf_op jit(solution)/shard_map/dot_general | solution.py:21
  240.2 7.1 %fusion.20 = f32[2,40,128,128]{3,2,1,0:T(8,128)S(1)} fusion(f32[2,40,128,128]{3,2,1,0:T(8,128)S(1)} %fusion.18, f32[2,40,128,128]{3,2,1,0:T(8,128)S(1)} %fusion.94, f32[128,128]{1,0:T(8,128)S(1)} %fusion.76), kind=kOutput, calls=%fused_computation.31 | convolution fusion | flops 2015887360 | bytes 15794176 | tf_op jit(solution)/shard_map/dot_general | solution.py:24
  247.3 7.1 %fusion.21 = f32[2,40,128,128]{3,2,1,0:T(8,128)S(1)} fusion(f32[2,40,128,128]{3,2,1,0:T(8,128)S(1)} %fusion.19, f32[2,40,128,128]{3,2,1,0:T(8,128)S(1)} %fusion.94, f32[128,128]{1,0:T(8,128)S(1)} %fusion.76), kind=kOutput, calls=%fused_computation.32 | convolution fusion | flops 2015887360 | bytes 15794176 | tf_op jit(solution)/shard_map/dot_general | solution.py:25
  254.4 6.9 %fusion.95 = f32[2,40,128,128]{3,2,1,0:T(8,128)S(1)} fusion(f32[2,40,128,128]{3,2,1,0:T(8,128)S(1)} %fusion.21, f32[2,40,128,128]{3,2,1,0:T(8,128)S(1)} %fusion.20), kind=kOutput, calls=%fused_computation.102 | convolution fusion | flops 2013265920 | bytes 15728640 | tf_op jit(solution)/shard_map/dot_general | solution.py:21
  261.3 7.0 %broadcast_divide_fusion = f32[2,40,128,128]{3,2,1,0:T(8,128)S(1)} fusion(f32[2,40]{1,0:T(2,128)S(1)} %get-tuple-element.11, f32[2,40,128,128]{3,2,1,0:T(8,128)S(1)} %fusion.21, f32[2,40,128,128]{3,2,1,0:T(8,128)S(1)} %fusion.95, f32[128,128]{1,0:T(8,128)S(1)} %fusion.76), kind=kOutput, calls=%fused_computation.42 | convolution fusion | flops 2017198080 | bytes 15794496 | tf_op jit(solution)/shard_map/dot_general | solution.py:25
  272.5 8.3 %copy.22 = bf16[2,256,5120]{1,2,0:T(8,128)(2,1)} copy(bf16[2,256,5120]{2,1,0:T(8,128)(2,1)} %all-gather.4.cloned.1.call-done) | data formatting | bytes 10485760 | tf_op jit(solution)/shard_map/all_gather | solution.py:50
  280.8 5.7 %multiply_bitcast_fusion = f32[2,40,128,128]{2,3,0,1:T(8,128)S(1)} fusion(bf16[256,40,128,1]{2,1,0,3:T(8,128)(2,1)} %bitcast.87, bf16[2,256,40,128]{1,3,2,0:T(8,128)(2,1)} %bitcast.89), kind=kOutput, calls=%fused_computation.11 | convolution fusion | flops 672399360 | bytes 13107200 | tf_op jit(solution)/shard_map/athi,bthj->abhij/dot_general | solution.py:67
  286.6 6.8 %fusion.2 = f32[40,128,2,128]{3,1,0,2:T(8,128)} fusion(f32[2,40,128,128]{2,3,0,1:T(8,128)S(1)} %multiply_bitcast_fusion, f32[2,40,128,128]{3,2,1,0:T(8,128)S(1)} %bitcast.84), kind=kOutput, calls=%fused_computation.3 | convolution fusion | flops 2013265920 | bytes 13107200 | tf_op jit(solution)/shard_map/dot_general | solution.py:70
  293.4 47.4 %all-gather.6.cloned.1.call-done = f32[2,40,128,128]{3,2,1,0:T(8,128)} async-done(((f32[1,40,128,128]{3,2,1,0:T(8,128)}), f32[2,40,128,128]{3,2,1,0:T(8,128)}) %all-gather.6.cloned.1.call-update) | async-done | bytes 5242896 | tf_op jit(solution)/shard_map/all_gather | solution.py:60
  340.7 9.5 %fusion.57 = f32[1,2,40,128,128]{4,3,2,1,0:T(8,128)} fusion(f32[2,40,128,128]{3,2,1,0:T(8,128)} %all-gather.6.cloned.1.call-done, f32[40,128,2,128]{3,1,0,2:T(8,128)} %fusion.2), kind=kOutput, calls=%fused_computation.69 | convolution fusion | flops 2013265920 | bytes 15728640 | tf_op jit(solution)/shard_map/dot_general | solution.py:73
  350.3 4.5 all-gather
  354.8 6.1 %fusion.25 = f32[40,1,128]{2,1,0:T(1,128)S(1)} fusion(f32[40,128,1]{1,2,0:T(1,128)S(1)} %bitcast.94, f32[2,40,128,128]{3,2,1,0:T(8,128)} %copy-done.2), kind=kOutput, calls=%fused_computation.36 | convolution fusion | flops 7864320 | bytes 2662400 | tf_op jit(solution)/shard_map/ahij,ahj->ahi/dot_general | solution.py:76
  360.9 6.8 %fusion.96 = f32[2,40,1,128]{3,2,1,0:T(1,128)S(1)} fusion(f32[2,40,128,1]{2,3,1,0:T(1,128)S(1)} %bitcast.91, f32[2,40,128,128]{3,2,1,0:T(8,128)} %all-gather.6.cloned.1.call-done), kind=kOutput, calls=%fused_computation.103 | convolution fusion | flops 15728640 | bytes 5324800 | tf_op jit(solution)/shard_map/bhi,bhij->bhj/dot_general | solution.py:77
  367.7 61.2 %reduce-scatter.2.cloned.1.call-done = f32[1,2,40,8,128]{4,3,2,1,0:T(8,128)} async-done(((f32[1,2,40,128,128]{4,3,2,1,0:T(8,128)}), f32[1,2,40,8,128]{4,3,2,1,0:T(8,128)}) %reduce-scatter.2.cloned.1.call-update) | async-done | bytes 327696 | tf_op jit(solution)/shard_map/reduce_scatter | solution.py:75
  430.6 30.5 %psum.23 = f32[1,2,40]{2,1,0:T(2,128)S(1)} all-reduce(f32[1,2,40]{2,1,0:T(2,128)S(1)} %bitcast.96), channel_id=1, replica_groups=mesh['tok'=16,'lay'=2] {'tok'}, use_global_device_ids=true, to_apply=%region_7.0 | all-reduce | flops 80 | bytes 640 | tf_op jit(solution)/shard_map/psum | solution.py:82
  (41 shorter events, 12.7 us)
Async XLA Ops:
  8.0 136.7 %all-reduce.2.cloned.1.call-start = ((), (), s32[]{:S(2)}) async-start(), calls=%async_computation.1 | async-start | bytes 10485760 | tf_op jit(solution)/shard_map/psum | solution.py:53
  8.0 3.5 copy-start
  10.5 1.6 copy-start.3
  16.2 3.0 copy-start.1
  16.2 256.3 %all-gather.4.cloned.1.call-start = ((), (), s32[]{:S(2)}) async-start(), calls=%async_computation.2 | async-start | bytes 7864320 | tf_op jit(solution)/shard_map/all_gather | solution.py:50
  16.8 323.9 %all-gather.6.cloned.1.call-start = ((), (), s32[]{:S(2)}) async-start(), calls=%async_computation.3 | async-start | bytes 7864320 | tf_op jit(solution)/shard_map/all_gather | solution.py:60
  144.7 5.5 %copy-start.4 = (f32[2,1,40,128,128]{4,3,2,1,0:T(8,128)S(1)}, f32[2,1,40,128,128]{4,3,2,1,0:T(8,128)}, u32[]{:S(2)}) copy-start(f32[2,1,40,128,128]{4,3,2,1,0:T(8,128)} %all-reduce.2.cloned.1.call-done) | copy-start | bytes 15728644
  268.3 2.4 copy-start.2
  272.4 156.4 %reduce-scatter.2.cloned.1.call-start = ((), (), s32[]{:S(2)}) async-start(), calls=%async_computation.4 | async-start | bytes 5570560 | tf_op jit(solution)/shard_map/reduce_scatter | solution.py:75
  272.5 14.0 %slice-start = ((s8[5242880]{0:T(1024)(128)(4,1)}), s8[1048576]{0:T(1024)(128)(4,1)S(1)}, s32[]{:S(2)}) async-start(s8[5242880]{0:T(1024)(128)(4,1)} %bitcast.83), calls=%async_computation.5 | async-start | bytes 2097152
  280.8 5.8 %slice-start.1 = ((s8[5242880]{0:T(1024)(128)(4,1)}), s8[4194304]{0:T(1024)(128)(4,1)S(1)}, s32[]{:S(2)}) async-start(s8[5242880]{0:T(1024)(128)(4,1)} %bitcast.83), calls=%async_computation.6 | async-start | bytes 8388608
Sparse Core Ops, SparseCore 0:
  16.4 128.3 all-reduce.1
  350.4 78.4 reduce-scatter.1
Sparse Core Ops, SparseCore 1:
  18.3 71.1 all-gather.3
  272.5 68.2 all-gather.5
where the time goes:
time: 474 us; the launch traced here: 470 us
  waiting for transfers between devices  169 us (36%)
  matrix products  155 us (33%)
  blocking collectives  99.8 us (21%)
  between operations  16.3 us (3%)
  local copies, waits for them, and re-layouts  15.4 us (3%)
  other arithmetic  13.5 us (3%)
    psum x1, blocking collectives, local(): lax.psum((jnp.stack([gram_first, gram_second]), jnp.stack([sums_first, su...  64.8 us
    reduce_scatter x1, waiting for transfers between devices, local(): lax.psum_scatter(whitened_part, 'tok', scatter_dimension=3, tiled=True)  61.2 us
    psum x1, waiting for transfers between devices, local(): lax.psum((jnp.stack([gram_first, gram_second]), jnp.stack([sums_first, su...  60.2 us
    all_gather x1, waiting for transfers between devices, local(): lax.all_gather(whitening[1], 'lay', axis=0, tiled=True)  47.4 us
    dot_general x6, matrix products, newton_whiten(): jnp.matmul(factor_iter, inverse_iter, precision=top_precision)  41.6 us
    dot_general x6, matrix products, newton_whiten(): jnp.matmul(inverse_iter, square_iter, precision=top_precision)  40.3 us
    dot_general x5, matrix products, newton_whiten(): square_iter = jnp.matmul(square_iter, factor_iter, precision=top_precision)  36 us
    psum x1, blocking collectives, local(): lax.psum(jnp.sum(row_block * row_block, axis=(-2, -1)), 'tok') / HEAD_DIM  30.5 us
  transfers between devices with their start and end apart: 4, of which 3 were waited for; matrix products, arithmetic and copies ran while one was open for 34% of the time, Pallas kernels for 0%

commit v1 on v0

v1 whole, which is shorter than its diff:
```python
import functools

import jax
import jax.numpy as jnp
from jax import lax
from jax.experimental import pallas as pl
from jax.experimental.pallas import tpu as pltpu
from jax.sharding import PartitionSpec as P

HEADS = 40
HEAD_DIM = 128
ITERS = 6
PAD = 8

ridge_weight = 0.05
MESH = pl.DeviceIdType.MESH
HI = lax.Precision.HIGHEST


def dot_tt(a, b, precision=None):
    return lax.dot_general(
        a, b, (((0,), (0,)), ((), ())), preferred_element_type=jnp.float32, precision=precision
    )


def mm(a, b):
    return jnp.dot(a, b, preferred_element_type=jnp.float32, precision=HI)


def kernel(
    n, R, hp, token_total,
    x1, x2, out, simout,
    x2o, gp, gd, gy, gz, cp, cd, cy, cz, slab, wbuf, sbuf, yb, zb,
    x_s, x_r, gd_s, gd_r, gy_s, gy_r, gz_s, gz_r,
    cd_s, cd_r, cy_s, cy_r, cz_s, cz_r,
    p_s, p_r, q_s, q_r, az_s, az_r, ay_s, ay_r, ad_s, ad_r, ss_s, ss_r, o_s,
):
    me = lax.axis_index("tok")
    lay = lax.axis_index("lay")
    other = 1 - lay
    c = lax.rem(me, 2)
    y = lax.rem(me // 2, 2)
    z = me // 4
    rows = x1.shape[0]
    D = HEAD_DIM
    core_peer = z * 4 + y * 2 + (1 - c)
    y_peer = z * 4 + (1 - y) * 2 + c

    def z_peer(zt):
        return zt * 4 + y * 2 + c

    def rc(src, dst, s, r, tok, ly):
        return pltpu.make_async_remote_copy(
            src_ref=src, dst_ref=dst, send_sem=s, recv_sem=r,
            device_id=(tok, ly), device_id_type=MESH,
        )

    barrier = pltpu.get_barrier_semaphore()
    for k in range(1, n):
        pl.semaphore_signal(barrier, inc=1, device_id=(lax.rem(me + k, n), lay), device_id_type=MESH)
    pl.semaphore_signal(barrier, inc=1, device_id=(me, other), device_id_type=MESH)
    pl.semaphore_wait(barrier, n)

    zts = [lax.rem(z + 1 + i, R) for i in range(R)]
    sends = []

    padded = R * 2 * hp != HEADS
    width = x1.shape[1] // R if not padded else x1.shape[1]
    x_parts = []
    for i in range(R if not padded else 1):
        cols = pl.ds(pl.multiple_of(zts[i] * width, 128), width) if not padded else pl.ds(0, width)
        d = rc(x2.at[:, cols], x2o.at[:, cols], x_s.at[i], x_r.at[i], me, other)
        d.start()
        x_parts.append(d)
        sends.append(d)

    def head_cols(zt, yy, j):
        h = (zt * 2 + yy) * hp + j
        if padded:
            h = jnp.minimum(h, HEADS - 1)
        return pl.ds(pl.multiple_of(h * D, D), D)

    ones = jnp.ones((PAD, rows), jnp.bfloat16)

    g_d = []
    for i in range(R):
        zt = zts[i]

        def gram_body(j, carry, zt=zt):
            for yy in range(2):
                cols = head_cols(zt, yy, j)
                for k, ref in enumerate((x1, x2)):
                    v = ref[:, cols]
                    gp[k, zt, yy, j, :D, :] = dot_tt(v, v)
                    gp[k, zt, yy, j, D:, :] = jnp.dot(ones, v, preferred_element_type=jnp.float32)
            return carry

        lax.fori_loop(0, hp, gram_body, 0)
        d = rc(gp.at[1 - c, zt], gd.at[zt], gd_s.at[i], gd_r.at[i], core_peer, lay)
        d.start()
        g_d.append(d)
        sends.append(d)

    def y_phase(part, dbuf, ybuf, s, r, d_list):
        out_list = []
        for i in range(R):
            zt = zts[i]
            d_list[i].wait_recv()

            def add_body(j, carry, zt=zt):
                part[c, zt, 1 - y, j] = part[c, zt, 1 - y, j] + dbuf[zt, 1 - y, j]
                return carry

            lax.fori_loop(0, hp, add_body, 0)
            d = rc(part.at[c, zt, 1 - y], ybuf.at[zt], s.at[i], r.at[i], y_peer, lay)
            d.start()
            out_list.append(d)
            sends.append(d)
        return out_list

    def z_phase(part, dbuf, ybuf, zbuf, s, r, y_list):
        out_list = []
        for i in range(R):
            zt = zts[i]
            y_list[i].wait_recv()

            def add_body(j, carry, zt=zt):
                part[c, zt, y, j] = part[c, zt, y, j] + dbuf[zt, y, j] + ybuf[zt, j]
                return carry

            lax.fori_loop(0, hp, add_body, 0)
            if i < R - 1:
                d = rc(part.at[c, zt, y], zbuf.at[i], s.at[i], r.at[i], z_peer(zt), lay)
                d.start()
                out_list.append(d)
                sends.append(d)
        return out_list

    g_y = y_phase(gp, gd, gy, gy_s, gy_r, g_d)
    g_z = z_phase(gp, gd, gy, gz, gz_s, gz_r, g_y)

    for d in g_z:
        d.wait_recv()

    eye = (
        lax.broadcasted_iota(jnp.int32, (D, D), 0) == lax.broadcasted_iota(jnp.int32, (D, D), 1)
    ).astype(jnp.float32)
    scales = []
    for j in range(hp):
        total = gp[c, z, y, j]
        for i in range(R - 1):
            total = total + gz[i, j]
        mean = total[D:, :] / token_total
        slab[0, j, D:, :] = mean
        cov = total[:D, :] / token_total - dot_tt(mean, mean, HI) * (1.0 / PAD) + ridge_weight * eye
        norm2 = jnp.sum(jnp.sum(cov * cov, axis=1, keepdims=True), axis=0, keepdims=True)
        scale = jnp.sqrt(norm2)
        scales.append(scale)
        y0 = cov / scale
        f = 1.5 * eye - 0.5 * y0
        yb[j] = mm(y0, f)
        zb[j] = f

    def ns_body(t, carry):
        fs = [1.5 * eye - 0.5 * mm(zb[j], yb[j]) for j in range(hp)]
        for j in range(hp):
            yb[j] = mm(yb[j], fs[j])
            zb[j] = mm(fs[j], zb[j])
        return carry

    lax.fori_loop(1, ITERS - 1, ns_body, 0)
    for j in range(hp):
        f = 1.5 * eye - 0.5 * mm(zb[j], yb[j])
        w = mm(f, zb[j]) / jnp.sqrt(scales[j])
        slab[0, j, :D, :] = w
        wbuf[c, z, y, j] = w

    to_core = rc(slab.at[0], slab.at[1], p_s.at[0], p_r.at[0], core_peer, lay)
    to_lay = rc(slab.at[0], slab.at[2], q_s.at[0], q_r.at[0], me, other)
    to_core.start()
    to_lay.start()
    sends += [to_core, to_lay]

    a_z = []
    for i in range(R - 1):
        w_own = wbuf.at[c, z, y]
        d = rc(w_own, w_own, az_s.at[i], az_r.at[i], z_peer(zts[i]), lay)
        d.start()
        a_z.append(d)
        sends.append(d)

    def forward(e, zs):
        block = wbuf.at[c, zs, y]
        d = rc(block, block, ay_s.at[e], ay_r.at[e], y_peer, lay)
        d.start()
        f = rc(block, block, ad_s.at[2 * e], ad_r.at[2 * e], core_peer, lay)
        f.start()
        sends.extend([d, f])
        return d, f

    zss = [z] + [lax.rem(z + R - 1 - i, R) for i in range(R - 1)]
    a_y, a_d = [], []
    d, f = forward(0, z)
    a_y.append(d)
    a_d.append(f)

    c_d = []
    for i in range(R):
        zt = zts[i]
        if i < len(x_parts):
            x_parts[i].wait_recv()

        def cross_body(j, carry, zt=zt):
            for yy in range(2):
                cols = head_cols(zt, yy, j)
                v = x1[:, cols]
                cp[0, zt, yy, j] = dot_tt(v, x2[:, cols])
                cp[1, zt, yy, j] = dot_tt(v, x2o[:, cols])
            return carry

        lax.fori_loop(0, hp, cross_body, 0)
        d = rc(cp.at[1 - c, zt], cd.at[zt], cd_s.at[i], cd_r.at[i], core_peer, lay)
        d.start()
        c_d.append(d)
        sends.append(d)

    c_y = y_phase(cp, cd, cy, cy_s, cy_r, c_d)

    for i in range(R - 1):
        a_z[i].wait_recv()
        d, f = forward(i + 1, zss[i + 1])
        a_y.append(d)
        a_d.append(f)

    c_z = z_phase(cp, cd, cy, cz, cz_s, cz_r, c_y)

    for e in range(R):
        a_y[e].wait_recv()
        block = wbuf.at[c, zss[e], 1 - y]
        f = rc(block, block, ad_s.at[2 * e + 1], ad_r.at[2 * e + 1], core_peer, lay)
        f.start()
        a_d.append(f)
        sends.append(f)
    o1 = pltpu.make_async_copy(wbuf.at[c], out.at[c], o_s.at[0])
    o1.start()

    for d in c_z:
        d.wait_recv()
    to_core.wait_recv()
    to_lay.wait_recv()
    sub = lax.broadcasted_iota(jnp.int32, sbuf.shape[1:], 0)
    tile = jnp.zeros(sbuf.shape[1:], jnp.float32)
    for j in range(hp):
        total = cp[c, z, y, j]
        for i in range(R - 1):
            total = total + cz[i, j]
        left = slab[c, j]
        right = slab[1 + c, j]
        cross = total / token_total - dot_tt(left[D:, :], right[D:, :], HI) * (1.0 / PAD)
        white = mm(mm(left[:D, :], cross), right[:D, :])
        value = jnp.sum(jnp.sum(white * white, axis=1, keepdims=True), axis=0, keepdims=True) / HEAD_DIM
        tile = jnp.where(sub == j, value, tile)
    sbuf[me] = tile
    s_list = []
    for k in range(1, n):
        d = rc(sbuf.at[me], sbuf.at[me], ss_s.at[k], ss_r.at[k], lax.rem(me + k, n), lay)
        d.start()
        s_list.append(d)
        sends.append(d)

    for f in a_d:
        f.wait_recv()
    o2 = pltpu.make_async_copy(wbuf.at[1 - c], out.at[1 - c], o_s.at[1])
    o2.start()
    for d in s_list:
        d.wait_recv()
    simout[...] = sbuf[...]
    o1.wait()
    o2.wait()
    for d in sends:
        d.wait_send()


def solution(mesh):
    n = mesh.shape["tok"]
    R = n // 4
    hp = -(-HEADS // (n // 2))
    srows = -(-hp // 8) * 8
    D = HEAD_DIM
    E = D + PAD

    def local(first_acts, second_acts):
        _, rows, width = first_acts.shape
        token_total = float(rows * n)
        f32 = jnp.float32
        dma = lambda k: pltpu.SemaphoreType.DMA((max(k, 1),))
        out, sims = pl.pallas_call(
            functools.partial(kernel, n, R, hp, token_total),
            out_shape=(
                jax.ShapeDtypeStruct((2, R, 2, hp, D, D), f32),
                jax.ShapeDtypeStruct((n, srows, D), f32),
            ),
            in_specs=[pl.BlockSpec(memory_space=pltpu.VMEM)] * 2,
            out_specs=(
                pl.BlockSpec(memory_space=pltpu.MemorySpace.HBM),
                pl.BlockSpec(memory_space=pltpu.VMEM),
            ),
            scratch_shapes=[
                pltpu.VMEM((rows, width), jnp.bfloat16),
                pltpu.VMEM((2, R, 2, hp, E, D), f32),
                pltpu.VMEM((R, 2, hp, E, D), f32),
                pltpu.VMEM((R, hp, E, D), f32),
                pltpu.VMEM((R - 1, hp, E, D), f32),
                pltpu.VMEM((2, R, 2, hp, D, D), f32),
                pltpu.VMEM((R, 2, hp, D, D), f32),
                pltpu.VMEM((R, hp, D, D), f32),
                pltpu.VMEM((R - 1, hp, D, D), f32),
                pltpu.VMEM((3, hp, E, D), f32),
                pltpu.VMEM((2, R, 2, hp, D, D), f32),
                pltpu.VMEM((n, srows, D), f32),
                pltpu.VMEM((hp, D, D), f32),
                pltpu.VMEM((hp, D, D), f32),
                dma(R), dma(R),
                dma(R), dma(R), dma(R), dma(R), dma(R - 1), dma(R - 1),
                dma(R), dma(R), dma(R), dma(R), dma(R - 1), dma(R - 1),
                dma(1), dma(1), dma(1), dma(1),
                dma(R - 1), dma(R - 1), dma(R), dma(R), dma(2 * R), dma(2 * R),
                dma(n), dma(n),
                dma(2),
            ],
            compiler_params=pltpu.CompilerParams(
                collective_id=0, has_side_effects=True, vmem_limit_bytes=58 * 1024 * 1024
            ),
        )(first_acts[0], second_acts[0])
        whitening = out.reshape(2, R * 2 * hp, D, D)[:, None, :HEADS]
        s = sims[:, :hp, 0].reshape(R * 2, 2, hp).transpose(1, 0, 2).reshape(2, R * 2 * hp)[:, :HEADS]
        s = jnp.where(lax.axis_index("lay") == 0, s, s[::-1])
        return whitening, s[None]

    in_specs = (P("lay", "tok", None), P("lay", "tok", None))
    out_specs = (P(None, "lay", None, None, None), P("lay", None, None))
    return jax.shard_map(local, mesh=mesh, in_specs=in_specs, out_specs=out_specs, check_vma=False)
```

time: 474 us -> 134 us (0.28)
  waiting for transfers between devices: 169 us -> 0 us
  matrix products: 155 us -> 0 us
  Pallas kernels: 0 us -> 126 us
  blocking collectives: 99.8 us -> 0 us
  between operations: 16.3 us -> 0.65 us
  other arithmetic: 13.5 us -> 0.57 us
  local copies, waits for them, and re-layouts: 15.4 us -> 6.53 us
    dot_general x24 -> x0, matrix products: 155 us -> none  [the longest x6 41.6 us: newton_whiten(): jnp.matmul(factor_iter, inverse_iter, precision=top_precision)]
    pallas_call x0 -> x1, Pallas kernels: none -> 126 us  [local(): pl.pallas_call(functools.partial(kernel, n, R, hp, token_total), out_shap...]
    psum x2 -> x0, blocking collectives: 95.3 us -> none  [the longest x1 64.8 us: local(): lax.psum((jnp.stack([gram_first, gram_second]), jnp.stack([sums_first, su...]
    reduce_scatter x1 -> x0, waiting for transfers between devices: 61.2 us -> none  [local(): lax.psum_scatter(whitened_part, 'tok', scatter_dimension=3, tiled=True)]
    psum x1 -> x0, waiting for transfers between devices: 60.2 us -> none  [local(): lax.psum((jnp.stack([gram_first, gram_second]), jnp.stack([sums_first, su...]
    all_gather x2 -> x0, waiting for transfers between devices: 47.4 us -> none  [the longest x1 47.4 us: local(): lax.all_gather(whitening[1], 'lay', axis=0, tiled=True)]
    reduce_sum x4 -> x0, other arithmetic: 9.88 us -> none  [the longest x1 5.46 us: newton_whiten(): jnp.sum(matrices * matrices, axis=(-2, -1), keepdims=True)]
    all_gather x1 -> x0, local copies, waits for them, and re-layouts: 8.27 us -> none  [local(): gathered = lax.all_gather(second_acts, 'lay', axis=0, tiled=True)]
  transfers between devices with their start and end apart: 4 -> 0, of which waited for: 3 -> 0; matrix products, arithmetic and copies ran while one was open for 34% -> 0% of each run, Pallas kernels for 0% -> 0%
where the time goes in v1:
time: 134 us
  Pallas kernels  126 us (94%)
  local copies, waits for them, and re-layouts  6.53 us (5%)
    pallas_call x1, Pallas kernels, local(): pl.pallas_call(functools.partial(kernel, n, R, hp, token_total), out_shap...  126 us
    unnamed x1, local copies, waits for them, and re-layouts  5.49 us

profile of v1, /device:TPU:0, one launch (start us, length us, event | category | flops | bytes accessed | tf_op | source)
XLA Modules:
  0.0 134.1 jit_solution(603606445907018450)
XLA Ops:
  0.6 126.4 %shard_map.41 = (f32[2,4,2,5,128,128]{5,4,3,2,1,0:T(8,128)}, f32[16,8,128]{2,1,0:T(8,128)}) custom-call(bf16[256,5120]{1,0:T(8,128)(2,1)} %bitcast.11, bf16[256,5120]{1,0:T(8,128)(2,1)} %bitcast.12), custom_call_target="tpu_custom_call" | custom-call | tf_op jit(solution)/shard_map/pallas_call | solution.py:297
  127.0 0.9 slice_reduce_fusion
  127.9 0.1 reshape.7
  128.1 0.6 select_bitcast_fusion
  128.6 5.5 %copy.9 = f32[2,1,40,128,128]{4,3,2,1,0:T(8,128)} copy(f32[2,1,40,128,128]{4,3,2,1,0:T(8,128)} %bitcast.10) | data formatting | bytes 10485760
  (2 shorter events, 0.0 us)

commit v2 on v1

--- a/solution.py
+++ b/solution.py
@@ -27,10 +27,47 @@
     return jnp.dot(a, b, preferred_element_type=jnp.float32, precision=HI)
 
 
+BLOCKS = HEAD_DIM // 8
+KEPT = BLOCKS // 2 + 1
+PACKED = 8 * KEPT
+
+
+def lane_block():
+    return lax.broadcasted_iota(jnp.int32, (8, HEAD_DIM), 1) // 8
+
+
+def pack(a):
+    lb = lane_block()
+    xs = [a[8 * e : 8 * e + 8, :] for e in range(BLOCKS)]
+    step = 1
+    while step < BLOCKS:
+        bit = (lb // step) % 2 == 1
+        xs = [jnp.where(bit, xs[(e + step) % BLOCKS], xs[e]) for e in range(BLOCKS)]
+        step *= 2
+    return jnp.concatenate([xs[(-d) % BLOCKS] for d in range(KEPT)], axis=0)
+
+
+def unpack(p):
+    lb = lane_block()
+    zero = jnp.zeros((8, HEAD_DIM), jnp.float32)
+    ys = [zero] * BLOCKS
+    for d in range(KEPT):
+        ys[(-d) % BLOCKS] = p[8 * d : 8 * d + 8, :]
+    step = 1
+    while step < BLOCKS:
+        bit = (lb // step) % 2 == 1
+        ys = [jnp.where(bit, ys[(e - step) % BLOCKS], ys[e]) for e in range(BLOCKS)]
+        step *= 2
+    half = jnp.concatenate(ys, axis=0)
+    rb = lax.broadcasted_iota(jnp.int32, (HEAD_DIM, HEAD_DIM), 0) // 8
+    cb = lax.broadcasted_iota(jnp.int32, (HEAD_DIM, HEAD_DIM), 1) // 8
+    return jnp.where((cb - rb + BLOCKS) % BLOCKS < KEPT, half, half.T)
+
+
 def kernel(
     n, R, hp, token_total,
     x1, x2, out, simout,
-    x2o, gp, gd, gy, gz, cp, cd, cy, cz, slab, wbuf, sbuf, yb, zb,
+    x2o, gp, gd, gy, gz, cp, cd, cys, cy, czs, cz, slab, wbuf, wfull, sbuf, yb, zb,
     x_s, x_r, gd_s, gd_r, gy_s, gy_r, gz_s, gz_r,
     cd_s, cd_r, cy_s, cy_r, cz_s, cz_r,
     p_s, p_r, q_s, q_r, az_s, az_r, ay_s, ay_r, ad_s, ad_r, ss_s, ss_r, o_s,
@@ -91,8 +128,8 @@
                 cols = head_cols(zt, yy, j)
                 for k, ref in enumerate((x1, x2)):
                     v = ref[:, cols]
-                    gp[k, zt, yy, j, :D, :] = dot_tt(v, v)
-                    gp[k, zt, yy, j, D:, :] = jnp.dot(ones, v, preferred_element_type=jnp.float32)
+                    gp[k, zt, yy, j, :PACKED, :] = pack(dot_tt(v, v))
+                    gp[k, zt, yy, j, PACKED:, :] = jnp.dot(ones, v, preferred_element_type=jnp.float32)
             return carry
 
         lax.fori_loop(0, hp, gram_body, 0)
@@ -137,7 +174,69 @@
         return out_list
 
     g_y = y_phase(gp, gd, gy, gy_s, gy_r, g_d)
+
+    def c_d(i):
+        return rc(cp.at[1 - c, zts[i]], cd.at[zts[i]], cd_s.at[i], cd_r.at[i], core_peer, lay)
+
+    def c_y(i):
+        return rc(cys.at[zts[i]], cy.at[zts[i]], cy_s.at[i], cy_r.at[i], y_peer, lay)
+
+    def c_z(i):
+        return rc(czs.at[zts[i]], cz.at[i], cz_s.at[i], cz_r.at[i], z_peer(zts[i]), lay)
+
+    def cross_chunk(k, ref, i):
+        zt = zts[i]
+
+        def body(j, carry):
+            for yy in range(2):
+                cols = head_cols(zt, yy, j)
+                cp[k, zt, yy, j] = dot_tt(x1[:, cols], ref[:, cols])
+            return carry
+
+        lax.fori_loop(0, hp, body, 0)
+
+        @pl.when(c == 1 - k)
+        def _():
+            c_d(i).start()
+
+    def cross_y(k):
+        @pl.when(c == k)
+        def _():
+            for i in range(R):
+                zt = zts[i]
+                c_d(i).wait_recv()
+
+                def body(j, carry, zt=zt):
+                    total = cp[k, zt, 1 - y, j] + cd[zt, 1 - y, j]
+                    cys[zt, j] = total
+                    return carry
+
+                lax.fori_loop(0, hp, body, 0)
+                c_y(i).start()
+
+    def cross_z(k):
+        @pl.when(c == k)
+        def _():
+            for i in range(R):
+                zt = zts[i]
+                c_y(i).wait_recv()
+
+                def body(j, carry, zt=zt, last=i == R - 1):
+                    total = cp[k, zt, y, j] + cd[zt, y, j] + cy[zt, j]
+                    if last:
+                        cp[k, zt, y, j] = total
+                    else:
+                        czs[zt, j] = total
+                    return carry
+
+                lax.fori_loop(0, hp, body, 0)
+                if i < R - 1:
+                    c_z(i).start()
+
+    for i in range(R):
+        cross_chunk(0, x2, i)
     g_z = z_phase(gp, gd, gy, gz, gz_s, gz_r, g_y)
+    cross_y(0)
 
     for d in g_z:
         d.wait_recv()
@@ -150,9 +249,9 @@
         total = gp[c, z, y, j]
         for i in range(R - 1):
             total = total + gz[i, j]
-        mean = total[D:, :] / token_total
+        mean = total[PACKED:, :] / token_total
         slab[0, j, D:, :] = mean
-        cov = total[:D, :] / token_total - dot_tt(mean, mean, HI) * (1.0 / PAD) + ridge_weight * eye
+        cov = unpack(total[:PACKED, :]) / token_total - dot_tt(mean, mean, HI) * (1.0 / PAD) + ridge_weight * eye
         norm2 = jnp.sum(jnp.sum(cov * cov, axis=1, keepdims=True), axis=0, keepdims=True)
         scale = jnp.sqrt(norm2)
         scales.append(scale)
@@ -173,7 +272,8 @@
         f = 1.5 * eye - 0.5 * mm(zb[j], yb[j])
         w = mm(f, zb[j]) / jnp.sqrt(scales[j])
         slab[0, j, :D, :] = w
-        wbuf[c, z, y, j] = w
+        wbuf[c, z, y, j] = pack(w)
+        wfull[c, z, y, j] = w
 
     to_core = rc(slab.at[0], slab.at[1], p_s.at[0], p_r.at[0], core_peer, lay)
     to_lay = rc(slab.at[0], slab.at[2], q_s.at[0], q_r.at[0], me, other)
@@ -204,27 +304,29 @@
     a_y.append(d)
     a_d.append(f)
 
-    c_d = []
+    outs = []
+
+    def emit(cc, zs, yy):
+        d = pltpu.make_async_copy(wfull.at[cc, zs, yy], out.at[cc, zs, yy], o_s.at[len(outs)])
+        d.start()
+        outs.append(d)
+
+    def expand(cc, zs, yy):
+        def body(j, carry):
+            wfull[cc, zs, yy, j] = unpack(wbuf[cc, zs, yy, j])
+            return carry
+
+        lax.fori_loop(0, hp, body, 0)
+        emit(cc, zs, yy)
+
+    emit(c, z, y)
+    cross_z(0)
+
     for i in range(R):
-        zt = zts[i]
         if i < len(x_parts):
             x_parts[i].wait_recv()
-
-        def cross_body(j, carry, zt=zt):
-            for yy in range(2):
-                cols = head_cols(zt, yy, j)
-                v = x1[:, cols]
-                cp[0, zt, yy, j] = dot_tt(v, x2[:, cols])
-                cp[1, zt, yy, j] = dot_tt(v, x2o[:, cols])
-            return carry
-
-        lax.fori_loop(0, hp, cross_body, 0)
-        d = rc(cp.at[1 - c, zt], cd.at[zt], cd_s.at[i], cd_r.at[i], core_peer, lay)
-        d.start()
-        c_d.append(d)
-        sends.append(d)
-
-    c_y = y_phase(cp, cd, cy, cy_s, cy_r, c_d)
+        cross_chunk(1, x2o, i)
+    cross_y(1)
 
     for i in range(R - 1):
         a_z[i].wait_recv()
@@ -232,8 +334,10 @@
         a_y.append(d)
         a_d.append(f)
 
-    c_z = z_phase(cp, cd, cy, cz, cz_s, cz_r, c_y)
-
+    cross_z(1)
+
+    for e in range(1, R):
+        expand(c, zss[e], y)
     for e in range(R):
         a_y[e].wait_recv()
         block = wbuf.at[c, zss[e], 1 - y]
@@ -241,11 +345,10 @@
         f.start()
         a_d.append(f)
         sends.append(f)
-    o1 = pltpu.make_async_copy(wbuf.at[c], out.at[c], o_s.at[0])
-    o1.start()
-
-    for d in c_z:
-        d.wait_recv()
+        expand(c, zss[e], 1 - y)
+
+    for i in range(R - 1):
+        c_z(i).wait_recv()
     to_core.wait_recv()
     to_lay.wait_recv()
     sub = lax.broadcasted_iota(jnp.int32, sbuf.shape[1:], 0)
@@ -268,17 +371,24 @@
         s_list.append(d)
         sends.append(d)
 
-    for f in a_d:
-        f.wait_recv()
-    o2 = pltpu.make_async_copy(wbuf.at[1 - c], out.at[1 - c], o_s.at[1])
-    o2.start()
+    for e in range(R):
+        a_d[e].wait_recv()
+        expand(1 - c, zss[e], y)
+    for e in range(R):
+        a_d[R + e].wait_recv()
+        expand(1 - c, zss[e], 1 - y)
     for d in s_list:
         d.wait_recv()
     simout[...] = sbuf[...]
-    o1.wait()
-    o2.wait()
+    for d in outs:
+        d.wait()
     for d in sends:
         d.wait_send()
+    for i in range(R):
+        c_d(i).wait_send()
+        c_y(i).wait_send()
+    for i in range(R - 1):
+        c_z(i).wait_send()
 
 
 def solution(mesh):
@@ -287,7 +397,7 @@
     hp = -(-HEADS // (n // 2))
     srows = -(-hp // 8) * 8
     D = HEAD_DIM
-    E = D + PAD
+    E = PACKED + PAD
 
     def local(first_acts, second_acts):
         _, rows, width = first_acts.shape
@@ -314,8 +424,11 @@
                 pltpu.VMEM((2, R, 2, hp, D, D), f32),
                 pltpu.VMEM((R, 2, hp, D, D), f32),
                 pltpu.VMEM((R, hp, D, D), f32),
+                pltpu.VMEM((R, hp, D, D), f32),
+                pltpu.VMEM((R, hp, D, D), f32),
                 pltpu.VMEM((R - 1, hp, D, D), f32),
-                pltpu.VMEM((3, hp, E, D), f32),
+                pltpu.VMEM((3, hp, D + PAD, D), f32),
+                pltpu.VMEM((2, R, 2, hp, PACKED, D), f32),
                 pltpu.VMEM((2, R, 2, hp, D, D), f32),
                 pltpu.VMEM((n, srows, D), f32),
                 pltpu.VMEM((hp, D, D), f32),
@@ -326,7 +439,7 @@
                 dma(1), dma(1), dma(1), dma(1),
                 dma(R - 1), dma(R - 1), dma(R), dma(R), dma(2 * R), dma(2 * R),
                 dma(n), dma(n),
-                dma(2),
+                dma(4 * R),
             ],
             compiler_params=pltpu.CompilerParams(
                 collective_id=0, has_side_effects=True, vmem_limit_bytes=58 * 1024 * 1024

time: 134 us -> 113 us (0.84); the launches traced: 134 us -> 111 us
  Pallas kernels: 126 us -> 103 us
    pallas_call x1, Pallas kernels: 126 us -> 103 us  [local(): pl.pallas_call(functools.partial(kernel, n, R, hp, token_total), out_shap...]
where the time goes in v2:
time: 113 us; the launch traced here: 111 us
  Pallas kernels  103 us (91%)
  local copies, waits for them, and re-layouts  6.53 us (6%)
    pallas_call x1, Pallas kernels, local(): pl.pallas_call(functools.partial(kernel, n, R, hp, token_total), out_shap...  103 us
    unnamed x1, local copies, waits for them, and re-layouts  5.49 us

profile of v2, /device:TPU:0, one launch (start us, length us, event | category | flops | bytes accessed | tf_op | source)
XLA Modules:
  0.0 110.7 jit_solution(7356466058410058760)
XLA Ops:
  0.6 102.9 %shard_map.41 = (f32[2,4,2,5,128,128]{5,4,3,2,1,0:T(8,128)}, f32[16,8,128]{2,1,0:T(8,128)}) custom-call(bf16[256,5120]{1,0:T(8,128)(2,1)} %bitcast.11, bf16[256,5120]{1,0:T(8,128)(2,1)} %bitcast.12), custom_call_target="tpu_custom_call" | custom-call | tf_op jit(solution)/shard_map/pallas_call | solution.py:407
  103.6 0.9 slice_reduce_fusion
  104.5 0.1 reshape.7
  104.6 0.6 select_bitcast_fusion
  105.2 5.5 %copy.9 = f32[2,1,40,128,128]{4,3,2,1,0:T(8,128)} copy(f32[2,1,40,128,128]{4,3,2,1,0:T(8,128)} %bitcast.10) | data formatting | bytes 10485760
  (2 shorter events, 0.0 us)
